TPU v7x, 32 devices: a whole 2x2x4 slice. The times are simulated.
32 devices in a mesh: tile: 16 (over z, y, core), cam: 2 (over x).
Axes of the slice: x: 2, y: 2, z: 4, core: 2. Of those that a mesh axis runs over, the one named last changes fastest.
Arguments:
- features: bfloat16 [6144, 256], P(('tile', 'cam')), may hold values from -6 to 6
- value_weight: bfloat16 [256, 256], replicated, may hold values from -0.375 to 0.375
- output_weight: bfloat16 [256, 256], replicated, may hold values from -0.375 to 0.375
- hit_list: int32 [16, 2], P('tile'), may hold values from 0 to 5, as said below
- sample_index: int32 [8192, 2, 64], P('tile'), may hold values from 0 to 1023, as said below
- attention: bfloat16 [8192, 64], P('tile'), may hold values from 0.0099487305 to 1
- validity: int32 [8192, 2], P('tile'), may hold values from 0 to 1, as said below
Outputs:
- projected: bfloat16 [8192, 256], P(('tile', 'cam'))
Inputs may be any that keep to these rules, and one draw needn't show every extreme that they name: `hit_list`: camera numbers 0 to 5; where a tile sees one camera its two entries are equal. `validity`: where a tile's two hit_list entries are equal, the second column is 0 for every query of that tile. `sample_index`: for one query, slot and head, the 8 entries h * 8 to h * 8 + 7 all differ.
All inputs are finite; a program needn't handle non-finite values.
Results may differ from a plain program's by a relative error of at most 0.0058.
Values may be sent and summed in bfloat16 or wider, within the bound.
A program may use at most 64 MiB of HBM per device.

v0:
```python
import jax
import jax.numpy as jnp
from jax import lax
from jax.sharding import PartitionSpec as P

D = 256
H = 8
K = 8
HITS = 2
CAM_ROWS = 1024


lane_width = 128
block_limit = 1 << 22


def request_table(hit_row, sample_index, attention, validity):
    queries = sample_index.shape[0]
    targets = hit_row[None, :, None] * CAM_ROWS + sample_index
    targets = (
        targets.reshape(queries, HITS, H, K).transpose(0, 2, 1, 3).reshape(queries, H, HITS * K)
    )
    hit_count = jnp.sum(validity, axis=1)
    inverse = 1.0 / jnp.maximum(hit_count, 1).astype(jnp.float32)
    weights = (
        attention.astype(jnp.float32).reshape(queries, 1, H, K)
        * validity.astype(jnp.float32)[:, :, None, None]
    )
    weights = weights * inverse[:, None, None, None]
    weights = weights.transpose(0, 2, 1, 3).reshape(queries, H, HITS * K).astype(jnp.bfloat16)
    return (targets, weights)


def sample_piece(running, section, first_row, positions, weights):
    row_count, width = section.shape
    queries = positions.shape[0]
    offset = first_row % lane_width
    groups = (row_count + lane_width - 1) // lane_width + 1
    buffer = jnp.zeros((groups * lane_width, width), section.dtype)
    buffer = lax.dynamic_update_slice_in_dim(buffer, section, offset, 0)
    high_part = positions // lane_width
    low_hot = ((positions % lane_width)[..., None] == jnp.arange(lane_width)).astype(jnp.bfloat16)
    per_block = max(1, block_limit // (queries * H * lane_width))
    block_groups = 1
    for candidate in range(min(groups, per_block), 0, -1):
        if groups % candidate == 0:
            block_groups = candidate
            break

    def one_block(block_id, summed):
        first_group = block_id * block_groups

        def compute(partial_value):
            high_hot = jnp.where(
                high_part[..., None] - first_group == jnp.arange(block_groups),
                weights[..., None],
                jnp.zeros((), jnp.bfloat16),
            )
            mixing = jnp.einsum(
                "qhsa,qhsb->qhab", high_hot, low_hot, preferred_element_type=jnp.float32
            )
            mixing = mixing.reshape(queries, H, block_groups * lane_width).astype(jnp.bfloat16)
            block_values = lax.dynamic_slice_in_dim(
                buffer, first_group * lane_width, block_groups * lane_width, 0
            )
            block_values = block_values.reshape(block_groups * lane_width, H, width // H)
            return partial_value + jnp.einsum(
                "qhr,rhd->qhd", mixing, block_values, preferred_element_type=jnp.float32
            )

        def keep_same(partial_value):
            return partial_value

        inside = (
            (high_part >= first_group) & (high_part < first_group + block_groups) & (weights != 0)
        )
        return lax.cond(jnp.any(inside), compute, keep_same, summed)

    return lax.fori_loop(0, groups // block_groups, one_block, running)


def body(features, value_weight, output_weight, hit_list, sample_index, attention, validity):
    values = jnp.dot(features, value_weight, preferred_element_type=jnp.float32).astype(
        jnp.bfloat16
    )
    cam_total = lax.axis_size("cam")
    cam_place = lax.axis_index("cam")
    tile_queries = sample_index.shape[0]
    share_rows = tile_queries // cam_total
    query_start = cam_place * share_rows
    local_index = lax.dynamic_slice_in_dim(sample_index, query_start, share_rows, 0)
    local_attention = lax.dynamic_slice_in_dim(attention, query_start, share_rows, 0)
    local_validity = lax.dynamic_slice_in_dim(validity, query_start, share_rows, 0)
    targets, weights = request_table(hit_list[0], local_index, local_attention, local_validity)
    empty = jnp.zeros((share_rows, H, D // H), jnp.float32)
    sampled = sample_piece(
        empty,
        lax.all_gather(values, ("tile", "cam"), axis=0, tiled=True),
        jnp.int32(0),
        targets,
        weights,
    )
    sampled = sampled.reshape(share_rows, D)
    attended = sampled.astype(jnp.bfloat16)
    return jnp.dot(attended, output_weight, preferred_element_type=jnp.float32).astype(jnp.bfloat16)


def solution(mesh):
    in_specs = (
        P(("tile", "cam"), None),
        P(),
        P(),
        P("tile", None),
        P("tile", None, None),
        P("tile", None),
        P("tile", None),
    )
    out_specs = P(("tile", "cam"), None)
    return jax.shard_map(body, mesh=mesh, in_specs=in_specs, out_specs=out_specs, check_vma=False)
```

profile of v0, /device:TPU:13, one launch (start us, length us, event | category | flops | bytes accessed | tf_op | source)
XLA Modules:
  0.0 229.5 jit_solution(6184201895812826939)
XLA Ops:
  6.5 0.0 copy-start
  6.5 0.0 all-gather.2.cloned.1.call-start
  6.5 1.8 convolution_convert_fusion.1
  8.3 0.0 all-gather.2.cloned.1.call-update
  8.4 0.7 multiply_bitcast_fusion
  9.0 1.1 add_select_fusion
  10.1 0.4 copy.23
  10.5 0.7 dynamic-slice_reduce_fusion
  11.3 0.8 bitcast_convert_fusion
  12.0 57.8 %all-gather.2.cloned.1.call-done = bf16[6144,256]{1,0:T(8,128)(2,1)} async-done(((bf16[192,256]{1,0:T(8,128)(2,1)}), bf16[6144,256]{1,0:T(8,128)(2,1)}) %all-gather.2.cloned.1.call-update) | async-done | bytes 3145744 | tf_op jit(solution)/shard_map/all_gather | solution.py:98
  69.9 4.7 %copy.24 = bf16[6144,256]{0,1:T(8,128)(2,1)} copy(bf16[6144,256]{1,0:T(8,128)(2,1)} %all-gather.2.cloned.1.call-done) | data formatting | bytes 6291456
  74.5 3.8 %dynamic_update_slice.3.clone = bf16[6272,256]{0,1:T(8,128)(2,1)} pad(bf16[6144,256]{0,1:T(8,128)(2,1)} %copy.24, bf16[]{:T(256)} %constant.95.clone.1), padding=0_128x0_0 | pad | bytes 6356994 | tf_op jit(solution)/shard_map/dynamic_update_slice | solution.py:40
  78.3 0.7 broadcast_in_dim.10
  79.1 141.7 %while.17 = (s32[]{:T(128)}, f32[256,8,32]{0,2,1:T(8,128)}, s32[256,8,16]{0,2,1:T(8,128)S(1)}, bf16[6272,256]{0,1:T(8,128)(2,1)}, f32[256,8,8]{0,2,1:T(8,128)S(1...) while((s32[]{:T(128)}, f32[256,8,32]{0,2,1:T(8,128)}, ...), condition=%wide.region_5.6_spmd.clone, body=%wide.region_1.5_spmd.clone.sunk | while | flops 187301888 | bytes 34620664 | solution.py:79
  79.1 0.7 and_reduce_fusion.2
  80.4 6.5 %fusion.36 = bf16[256,8,16,128]{3,2,1,0:T(8,128)(2,1)} fusion(s32[256,8,16]{2,1,0:T(8,128)S(1)} %get-tuple-element.302), kind=kLoop, calls=%fused_computation.17.clone.1 | loop fusion | flops 8388608 | bytes 8519680 | tf_op jit(solution)/shard_map/convert_element_type | solution.py:42
  86.9 21.7 %conditional.3 = (f32[256,8,32]{0,2,1:T(8,128)}) conditional(s32[]{:T(128)} %convert_element_type.70, f32[256,8,32]{0,2,1:T(8,128)} %get-tuple-element.286, (s32[]{:T(128)}, bf16[6272,256]{0,1:T(8,128)(2,1)}, s32[256,8,16]{0,2,1:T(8,128)S(1)}, bf16[256,8,16]{0,2,1:T(8,128)(2,1)S(1)}, bf16[256,8,16,128]{3,2,1,0:T(8,128)(2,1)}, ...), branch_computations={%region_3.3_spmd, %region_4.4_spmd} | conditional | flops 178552832 | bytes 25821246 | solution.py:77
  86.9 1.1 constant_dynamic-slice_fusion
  88.0 0.3 copy.20
  88.3 0.4 copy.19
  88.7 0.1 broadcast_subtract_fusion
  88.8 7.7 %fusion.10 = bf16[256,8,7,128]{3,2,1,0:T(8,128)(2,1)} fusion(bf16[256,8,16,128]{3,2,1,0:T(8,128)(2,1)} %get-tuple-element.131, s32[256,8,16]{2,1,0:T(8,128)S(1)} %broadcast_subtract_fusion, bf16[256,8,16]{2,1,0:T(8,128)(2,1)S(1)} %copy.20), kind=kOutput, calls=%fused_computation.8 | convolution fusion | flops 61014016 | bytes 12255232 | tf_op jit(solution)/shard_map/while/body/eval_jaxpr/cond/branch_1_fun/qhsa,qhsb->qhab/dot_general | solution.py:59
  96.5 8.1 %convert_element_type.32 = bf16[256,8,896]{2,1,0:T(8,128)(2,1)} reshape(bf16[256,8,7,128]{3,2,1,0:T(8,128)(2,1)} %fusion.10) | data formatting | bytes 7340032 | tf_op jit(solution)/shard_map/while/body/eval_jaxpr/cond/branch_1_fun/convert_element_type | solution.py:62
  104.6 4.0 %fusion.18 = f32[256,8,32]{0,2,1:T(8,128)} fusion(f32[256,8,32]{0,2,1:T(8,128)} %get-tuple-element.126, bf16[896,8,32]{0,2,1:T(8,128)(2,1)S(1)} %bitcast.57, bf16[256,8,896]{2,1,0:T(8,128)(2,1)} %convert_element_type.32), kind=kOutput, calls=%fused_computation.12 | convolution fusion | flops 117506048 | bytes 4653056 | tf_op jit(solution)/shard_map/while/body/eval_jaxpr/cond/branch_1_fun/qhr,rhd->qhd/dot_general | solution.py:67
  108.6 0.7 and_reduce_fusion.2
  109.9 6.5 %fusion.36 = bf16[256,8,16,128]{3,2,1,0:T(8,128)(2,1)} fusion(s32[256,8,16]{2,1,0:T(8,128)S(1)} %get-tuple-element.302), kind=kLoop, calls=%fused_computation.17.clone.1 | loop fusion | flops 8388608 | bytes 8519680 | tf_op jit(solution)/shard_map/convert_element_type | solution.py:42
  116.4 21.7 %conditional.3 = (f32[256,8,32]{0,2,1:T(8,128)}) conditional(s32[]{:T(128)} %convert_element_type.70, f32[256,8,32]{0,2,1:T(8,128)} %get-tuple-element.286, (s32[]{:T(128)}, bf16[6272,256]{0,1:T(8,128)(2,1)}, s32[256,8,16]{0,2,1:T(8,128)S(1)}, bf16[256,8,16]{0,2,1:T(8,128)(2,1)S(1)}, bf16[256,8,16,128]{3,2,1,0:T(8,128)(2,1)}, ...), branch_computations={%region_3.3_spmd, %region_4.4_spmd} | conditional | flops 178552832 | bytes 25821246 | solution.py:77
  116.4 1.1 constant_dynamic-slice_fusion
  117.5 0.3 copy.20
  117.8 0.4 copy.19
  118.2 0.1 broadcast_subtract_fusion
  118.3 7.7 %fusion.10 = bf16[256,8,7,128]{3,2,1,0:T(8,128)(2,1)} fusion(bf16[256,8,16,128]{3,2,1,0:T(8,128)(2,1)} %get-tuple-element.131, s32[256,8,16]{2,1,0:T(8,128)S(1)} %broadcast_subtract_fusion, bf16[256,8,16]{2,1,0:T(8,128)(2,1)S(1)} %copy.20), kind=kOutput, calls=%fused_computation.8 | convolution fusion | flops 61014016 | bytes 12255232 | tf_op jit(solution)/shard_map/while/body/eval_jaxpr/cond/branch_1_fun/qhsa,qhsb->qhab/dot_general | solution.py:59
  126.1 8.1 %convert_element_type.32 = bf16[256,8,896]{2,1,0:T(8,128)(2,1)} reshape(bf16[256,8,7,128]{3,2,1,0:T(8,128)(2,1)} %fusion.10) | data formatting | bytes 7340032 | tf_op jit(solution)/shard_map/while/body/eval_jaxpr/cond/branch_1_fun/convert_element_type | solution.py:62
  134.2 4.0 %fusion.18 = f32[256,8,32]{0,2,1:T(8,128)} fusion(f32[256,8,32]{0,2,1:T(8,128)} %get-tuple-element.126, bf16[896,8,32]{0,2,1:T(8,128)(2,1)S(1)} %bitcast.57, bf16[256,8,896]{2,1,0:T(8,128)(2,1)} %convert_element_type.32), kind=kOutput, calls=%fused_computation.12 | convolution fusion | flops 117506048 | bytes 4653056 | tf_op jit(solution)/shard_map/while/body/eval_jaxpr/cond/branch_1_fun/qhr,rhd->qhd/dot_general | solution.py:67
  138.1 0.7 and_reduce_fusion.2
  139.5 6.5 %fusion.36 = bf16[256,8,16,128]{3,2,1,0:T(8,128)(2,1)} fusion(s32[256,8,16]{2,1,0:T(8,128)S(1)} %get-tuple-element.302), kind=kLoop, calls=%fused_computation.17.clone.1 | loop fusion | flops 8388608 | bytes 8519680 | tf_op jit(solution)/shard_map/convert_element_type | solution.py:42
  146.0 21.7 %conditional.3 = (f32[256,8,32]{0,2,1:T(8,128)}) conditional(s32[]{:T(128)} %convert_element_type.70, f32[256,8,32]{0,2,1:T(8,128)} %get-tuple-element.286, (s32[]{:T(128)}, bf16[6272,256]{0,1:T(8,128)(2,1)}, s32[256,8,16]{0,2,1:T(8,128)S(1)}, bf16[256,8,16]{0,2,1:T(8,128)(2,1)S(1)}, bf16[256,8,16,128]{3,2,1,0:T(8,128)(2,1)}, ...), branch_computations={%region_3.3_spmd, %region_4.4_spmd} | conditional | flops 178552832 | bytes 25821246 | solution.py:77
  146.0 1.1 constant_dynamic-slice_fusion
  147.0 0.3 copy.20
  147.4 0.4 copy.19
  147.8 0.1 broadcast_subtract_fusion
  147.9 7.7 %fusion.10 = bf16[256,8,7,128]{3,2,1,0:T(8,128)(2,1)} fusion(bf16[256,8,16,128]{3,2,1,0:T(8,128)(2,1)} %get-tuple-element.131, s32[256,8,16]{2,1,0:T(8,128)S(1)} %broadcast_subtract_fusion, bf16[256,8,16]{2,1,0:T(8,128)(2,1)S(1)} %copy.20), kind=kOutput, calls=%fused_computation.8 | convolution fusion | flops 61014016 | bytes 12255232 | tf_op jit(solution)/shard_map/while/body/eval_jaxpr/cond/branch_1_fun/qhsa,qhsb->qhab/dot_general | solution.py:59
  155.6 8.1 %convert_element_type.32 = bf16[256,8,896]{2,1,0:T(8,128)(2,1)} reshape(bf16[256,8,7,128]{3,2,1,0:T(8,128)(2,1)} %fusion.10) | data formatting | bytes 7340032 | tf_op jit(solution)/shard_map/while/body/eval_jaxpr/cond/branch_1_fun/convert_element_type | solution.py:62
  163.7 4.0 %fusion.18 = f32[256,8,32]{0,2,1:T(8,128)} fusion(f32[256,8,32]{0,2,1:T(8,128)} %get-tuple-element.126, bf16[896,8,32]{0,2,1:T(8,128)(2,1)S(1)} %bitcast.57, bf16[256,8,896]{2,1,0:T(8,128)(2,1)} %convert_element_type.32), kind=kOutput, calls=%fused_computation.12 | convolution fusion | flops 117506048 | bytes 4653056 | tf_op jit(solution)/shard_map/while/body/eval_jaxpr/cond/branch_1_fun/qhr,rhd->qhd/dot_general | solution.py:67
  167.7 0.7 and_reduce_fusion.2
  169.0 6.5 %fusion.36 = bf16[256,8,16,128]{3,2,1,0:T(8,128)(2,1)} fusion(s32[256,8,16]{2,1,0:T(8,128)S(1)} %get-tuple-element.302), kind=kLoop, calls=%fused_computation.17.clone.1 | loop fusion | flops 8388608 | bytes 8519680 | tf_op jit(solution)/shard_map/convert_element_type | solution.py:42
  175.5 21.7 %conditional.3 = (f32[256,8,32]{0,2,1:T(8,128)}) conditional(s32[]{:T(128)} %convert_element_type.70, f32[256,8,32]{0,2,1:T(8,128)} %get-tuple-element.286, (s32[]{:T(128)}, bf16[6272,256]{0,1:T(8,128)(2,1)}, s32[256,8,16]{0,2,1:T(8,128)S(1)}, bf16[256,8,16]{0,2,1:T(8,128)(2,1)S(1)}, bf16[256,8,16,128]{3,2,1,0:T(8,128)(2,1)}, ...), branch_computations={%region_3.3_spmd, %region_4.4_spmd} | conditional | flops 178552832 | bytes 25821246 | solution.py:77
  175.5 1.1 constant_dynamic-slice_fusion
  176.6 0.3 copy.20
  176.9 0.4 copy.19
  177.3 0.1 broadcast_subtract_fusion
  177.4 7.7 %fusion.10 = bf16[256,8,7,128]{3,2,1,0:T(8,128)(2,1)} fusion(bf16[256,8,16,128]{3,2,1,0:T(8,128)(2,1)} %get-tuple-element.131, s32[256,8,16]{2,1,0:T(8,128)S(1)} %broadcast_subtract_fusion, bf16[256,8,16]{2,1,0:T(8,128)(2,1)S(1)} %copy.20), kind=kOutput, calls=%fused_computation.8 | convolution fusion | flops 61014016 | bytes 12255232 | tf_op jit(solution)/shard_map/while/body/eval_jaxpr/cond/branch_1_fun/qhsa,qhsb->qhab/dot_general | solution.py:59
  185.2 8.1 %convert_element_type.32 = bf16[256,8,896]{2,1,0:T(8,128)(2,1)} reshape(bf16[256,8,7,128]{3,2,1,0:T(8,128)(2,1)} %fusion.10) | data formatting | bytes 7340032 | tf_op jit(solution)/shard_map/while/body/eval_jaxpr/cond/branch_1_fun/convert_element_type | solution.py:62
  193.2 4.0 %fusion.18 = f32[256,8,32]{0,2,1:T(8,128)} fusion(f32[256,8,32]{0,2,1:T(8,128)} %get-tuple-element.126, bf16[896,8,32]{0,2,1:T(8,128)(2,1)S(1)} %bitcast.57, bf16[256,8,896]{2,1,0:T(8,128)(2,1)} %convert_element_type.32), kind=kOutput, calls=%fused_computation.12 | convolution fusion | flops 117506048 | bytes 4653056 | tf_op jit(solution)/shard_map/while/body/eval_jaxpr/cond/branch_1_fun/qhr,rhd->qhd/dot_general | solution.py:67
  197.2 0.7 and_reduce_fusion.2
  198.5 6.5 %fusion.36 = bf16[256,8,16,128]{3,2,1,0:T(8,128)(2,1)} fusion(s32[256,8,16]{2,1,0:T(8,128)S(1)} %get-tuple-element.302), kind=kLoop, calls=%fused_computation.17.clone.1 | loop fusion | flops 8388608 | bytes 8519680 | tf_op jit(solution)/shard_map/convert_element_type | solution.py:42
  205.1 0.7 and_reduce_fusion.2
  206.4 6.5 %fusion.36 = bf16[256,8,16,128]{3,2,1,0:T(8,128)(2,1)} fusion(s32[256,8,16]{2,1,0:T(8,128)S(1)} %get-tuple-element.302), kind=kLoop, calls=%fused_computation.17.clone.1 | loop fusion | flops 8388608 | bytes 8519680 | tf_op jit(solution)/shard_map/convert_element_type | solution.py:42
  212.9 0.7 and_reduce_fusion.2
  214.2 6.5 %fusion.36 = bf16[256,8,16,128]{3,2,1,0:T(8,128)(2,1)} fusion(s32[256,8,16]{2,1,0:T(8,128)S(1)} %get-tuple-element.302), kind=kLoop, calls=%fused_computation.17.clone.1 | loop fusion | flops 8388608 | bytes 8519680 | tf_op jit(solution)/shard_map/convert_element_type | solution.py:42
  220.8 1.0 convert_element_type.47
  221.7 0.0 copy-done
  221.7 0.9 convolution_convert_fusion
  (5 shorter events, 0.0 us)
Async XLA Ops:
  6.5 215.2 %copy-start = (bf16[256,256]{1,0:T(8,128)(2,1)S(1)}, bf16[256,256]{1,0:T(8,128)(2,1)}, u32[]{:S(2)}) copy-start(bf16[256,256]{1,0:T(8,128)(2,1)} %param.13) | copy-start | bytes 393220
  6.5 63.3 %all-gather.2.cloned.1.call-start = ((), (), s32[]{:S(2)}) async-start(), calls=%async_computation | async-start | bytes 3244032 | tf_op jit(solution)/shard_map/all_gather | solution.py:98
Sparse Core Ops, SparseCore 0:
  10.2 59.5 all-gather.1
where the time goes:
time: 232 us; the launch traced here: 229 us
  waiting for transfers between devices  57.8 us (25%)
  other arithmetic  55 us (24%)
  matrix products  49.6 us (21%)
  local copies, waits for them, and re-layouts  49.1 us (21%)
  between operations  13.4 us (6%)
  loops' own time  4.49 us (2%)
    all_gather x1, waiting for transfers between devices, body(): lax.all_gather(values, ('tile', 'cam'), axis=0, tiled=True)  57.8 us
    convert_element_type x7, other arithmetic, sample_piece(): ((positions % lane_width)[..., None] == jnp.arange(lane_width)).astype(jn...  45.7 us
    convert_element_type x4, local copies, waits for them, and re-layouts, compute(): mixing.reshape(queries, H, block_groups * lane_width).astype(jnp.bfloat16)  32.4 us
    dot_general x4, matrix products, compute(): jnp.einsum('qhsa,qhsb->qhab', high_hot, low_hot, preferred_element_type=j...  31 us
    dot_general x4, matrix products, compute(): jnp.einsum('qhr,rhd->qhd', mixing, block_values, preferred_element_type=j...  15.9 us
    unnamed x4, local copies, waits for them, and re-layouts  5.08 us
    reduce_or x7, other arithmetic, one_block(): return lax.cond(jnp.any(inside), compute, keep_same, summed)  4.84 us
  transfers between devices with their start and end apart: 1, of which 1 were waited for; matrix products, arithmetic and copies ran while one was open for 2% of the time, Pallas kernels for 0%

commit v1 on v0

v1 whole, which is shorter than its diff:
```python
import functools

import jax
import jax.numpy as jnp
from jax import lax
from jax.experimental import pallas as pl
from jax.experimental.pallas import tpu as pltpu
from jax.sharding import PartitionSpec as P

H = 8
K = 8
HITS = 2
CAM_ROWS = 1024
LANES = 128
MESH = pl.DeviceIdType.MESH


def gather_kernel(depth, v_ref, G, recv, sx, sup, sdn, sy, sc):
    me = lax.axis_index("tile")
    x = lax.axis_index("cam")
    core = lax.rem(me, 2)
    y = lax.rem(me // 2, 2)
    z = me // 4
    rows = v_ref.shape[1]

    def place(zz, yy, cc):
        return (zz * 2 + yy) * 2 + cc

    def block_of(zz, yy, cc, b):
        return place(zz, yy, cc) * 2 + b

    def span(blk):
        return pl.ds(pl.multiple_of(blk * rows, 16), rows)

    has_up = z < depth - 1
    has_down = z > 0
    x_peer = (me, 1 - x)
    y_peer = (place(z, 1 - y, core), x)
    c_peer = (place(z, y, 1 - core), x)
    up_peer = (place(jnp.minimum(z + 1, depth - 1), y, core), x)
    down_peer = (place(jnp.maximum(z - 1, 0), y, core), x)

    barrier = pltpu.get_barrier_semaphore()
    for peer in (x_peer, y_peer, c_peer):
        pl.semaphore_signal(barrier, inc=1, device_id=peer, device_id_type=MESH)

    @pl.when(has_up)
    def _():
        pl.semaphore_signal(barrier, inc=1, device_id=up_peer, device_id_type=MESH)

    @pl.when(has_down)
    def _():
        pl.semaphore_signal(barrier, inc=1, device_id=down_peer, device_id_type=MESH)

    pl.semaphore_wait(barrier, 3 + has_up.astype(jnp.int32) + has_down.astype(jnp.int32))

    def copy(src, blk, send, peer):
        return pltpu.make_async_remote_copy(
            src_ref=src,
            dst_ref=G.at[span(blk)],
            send_sem=send,
            recv_sem=recv.at[blk],
            device_id=peer,
            device_id_type=MESH,
        )

    def arrived(blk):
        copy(G.at[span(blk)], blk, sx.at[0], x_peer).wait_recv()

    own = block_of(z, y, core, x)
    copy(v_ref.at[1 - x], own, sx.at[0], x_peer).start()

    def send_up(src, blk, slot):
        copy(src, blk, sup.at[slot], up_peer).start()

    def send_down(src, blk, slot):
        copy(src, blk, sdn.at[slot], down_peer).start()

    def line_step(distance):
        for sign in (1, -1) if distance else (0,):
            zz = z - sign * distance
            live = (zz >= 0) & (zz < depth)
            for b in (0, 1):
                half = x if b == 0 else 1 - x

                def go(zz=zz, half=half, b=b, sign=sign):
                    blk = block_of(zz, y, core, half)
                    if distance == 0 and b == 0:
                        src = v_ref.at[x]
                    else:
                        arrived(blk)
                        src = G.at[span(blk)]
                    slot = zz * 2 + half
                    copy(src, blk, sy.at[slot], y_peer).start()
                    if sign >= 0:
                        pl.when(has_up)(lambda: send_up(src, blk, slot))
                    if sign <= 0:
                        pl.when(has_down)(lambda: send_down(src, blk, slot))
                    copy(src, blk, sc.at[slot], c_peer).start()

                if distance:
                    pl.when(live)(go)
                else:
                    go()

    def across_step(distance):
        for sign in (1, -1) if distance else (0,):
            zz = z - sign * distance
            live = (zz >= 0) & (zz < depth)
            for b in (0, 1):
                half = x if b == 0 else 1 - x

                def go(zz=zz, half=half):
                    blk = block_of(zz, 1 - y, core, half)
                    arrived(blk)
                    slot = depth * 2 + zz * 2 + half
                    copy(G.at[span(blk)], blk, sc.at[slot], c_peer).start()

                if distance:
                    pl.when(live)(go)
                else:
                    go()

    for distance in range(depth):
        line_step(distance)
        if distance:
            across_step(distance - 1)
    G[span(own), :] = v_ref[x]
    across_step(depth - 1)

    for zz in range(depth):
        for yy in (0, 1):
            for b in (0, 1):
                arrived(block_of(zz, yy, 1 - core, b))

    def sent(sem):
        copy(v_ref.at[0], own, sem, x_peer).wait_send()

    sent(sx.at[0])
    for slot in range(depth * 2):
        zz = slot // 2
        sent(sy.at[slot])
        pl.when(has_up & (zz <= z))(lambda slot=slot: sent(sup.at[slot]))
        pl.when(has_down & (zz >= z))(lambda slot=slot: sent(sdn.at[slot]))
    for slot in range(depth * 4):
        sent(sc.at[slot])


def gather_values(halves, tiles):
    depth = tiles // 4
    _, rows, width = halves.shape
    blocks = tiles * 2
    dma = pltpu.SemaphoreType.DMA
    return pl.pallas_call(
        functools.partial(gather_kernel, depth),
        out_shape=jax.ShapeDtypeStruct((blocks * rows, width), jnp.bfloat16),
        in_specs=[pl.BlockSpec(memory_space=pltpu.VMEM)],
        out_specs=pl.BlockSpec(memory_space=pltpu.VMEM),
        scratch_shapes=[
            dma((blocks,)),
            dma((1,)),
            dma((depth * 2,)),
            dma((depth * 2,)),
            dma((depth * 2,)),
            dma((depth * 4,)),
        ],
        compiler_params=pltpu.CompilerParams(collective_id=0, has_side_effects=True),
    )(halves)


def lane_pick(source, index):
    return jnp.take_along_axis(source, index, axis=1, mode="promise_in_bounds")


def sample_kernel(heads, hit_ref, vals_ref, idx_ref, attn_ref, factor_ref, out_ref, table, summed):
    width = vals_ref.shape[1]
    head_width = width // heads
    queries = idx_ref.shape[1]
    groups = queries // LANES
    parts = CAM_ROWS // LANES
    for s in range(HITS):
        for j in range(parts):
            first = pl.multiple_of(hit_ref[0, s] * CAM_ROWS + j * LANES, LANES)
            block = vals_ref[pl.ds(first, LANES), :].astype(jnp.float32)
            table[s * parts + j] = block.T

    def one(step, _):
        g = step // heads
        h = lax.rem(step, heads)
        lanes = pl.ds(pl.multiple_of(g * LANES, LANES), LANES)
        cols = pl.ds(pl.multiple_of(h * head_width, head_width), head_width)
        attn = attn_ref[pl.ds(pl.multiple_of(h * K, K), K), lanes]
        acc = jnp.zeros((head_width, LANES), jnp.float32)
        for s in range(HITS):
            index = idx_ref[pl.ds(pl.multiple_of(s * heads * K + h * K, K), K), lanes]
            low = index % LANES
            high = index // LANES
            weight = attn * factor_ref[s : s + 1, lanes]
            for k in range(K):
                lo = jnp.broadcast_to(low[k : k + 1], (head_width, LANES))
                hi = jnp.broadcast_to(high[k : k + 1], (head_width, LANES))
                picked = jnp.zeros((head_width, LANES), jnp.float32)
                for j in range(parts):
                    got = lane_pick(table[s * parts + j, cols, :], lo)
                    picked = jnp.where(hi == j, got, picked)
                acc = acc + weight[k : k + 1] * picked
        summed[cols, :] = acc

        @pl.when(h == heads - 1)
        def _():
            rows = pl.ds(pl.multiple_of(g * LANES, LANES), LANES)
            out_ref[rows, :] = summed[...].T.astype(out_ref.dtype)

        return 0

    lax.fori_loop(0, groups * heads, one, 0)


def sample(hit_list, vals, index, attention, validity, heads):
    queries = index.shape[0]
    width = vals.shape[1]
    padded = -(-queries // LANES) * LANES
    index = index.reshape(queries, HITS * heads * K).T
    attention = attention.astype(jnp.float32).T
    count = jnp.maximum(jnp.sum(validity, axis=1, keepdims=True), 1)
    factor = (validity.astype(jnp.float32) / count.astype(jnp.float32)).T
    pad = ((0, 0), (0, padded - queries))
    index, attention, factor = (jnp.pad(a, pad) for a in (index, attention, factor))
    out = pl.pallas_call(
        functools.partial(sample_kernel, heads),
        out_shape=jax.ShapeDtypeStruct((padded, width), jnp.bfloat16),
        in_specs=[pl.BlockSpec(memory_space=pltpu.SMEM)]
        + [pl.BlockSpec(memory_space=pltpu.VMEM)] * 4,
        out_specs=pl.BlockSpec(memory_space=pltpu.VMEM),
        scratch_shapes=[
            pltpu.VMEM((HITS * CAM_ROWS // LANES, width, LANES), jnp.float32),
            pltpu.VMEM((width, LANES), jnp.float32),
        ],
    )(hit_list, vals, index, attention, factor)
    return out[:queries]


def project_kernel(a_ref, w_ref, out_ref, other, send, recv):
    me = lax.axis_index("tile")
    x = lax.axis_index("cam")
    rows = out_ref.shape[0]
    width = a_ref.shape[1]
    peer = (me, 1 - x)
    barrier = pltpu.get_barrier_semaphore()
    pl.semaphore_signal(barrier, inc=1, device_id=peer, device_id_type=MESH)
    pl.semaphore_wait(barrier, 1)
    copy = pltpu.make_async_remote_copy(
        src_ref=a_ref.at[pl.ds(pl.multiple_of((1 - x) * rows, rows), rows)],
        dst_ref=other,
        send_sem=send,
        recv_sem=recv,
        device_id=peer,
        device_id_type=MESH,
    )
    copy.start()
    mine = a_ref[pl.ds(pl.multiple_of(x * rows, rows), rows), :]
    near = w_ref[pl.ds(pl.multiple_of(x * width, width), width), :]
    far = w_ref[pl.ds(pl.multiple_of((1 - x) * width, width), width), :]
    total = jnp.dot(mine, near, preferred_element_type=jnp.float32)
    copy.wait()
    total = total + jnp.dot(other[...], far, preferred_element_type=jnp.float32)
    out_ref[...] = total.astype(out_ref.dtype)


def project(attended, output_weight):
    rows = attended.shape[0] // 2
    return pl.pallas_call(
        project_kernel,
        out_shape=jax.ShapeDtypeStruct((rows, output_weight.shape[1]), jnp.bfloat16),
        in_specs=[pl.BlockSpec(memory_space=pltpu.VMEM)] * 2,
        out_specs=pl.BlockSpec(memory_space=pltpu.VMEM),
        scratch_shapes=[
            pltpu.VMEM((rows, attended.shape[1]), jnp.bfloat16),
            pltpu.SemaphoreType.DMA,
            pltpu.SemaphoreType.DMA,
        ],
        compiler_params=pltpu.CompilerParams(collective_id=1, has_side_effects=True),
    )(attended, output_weight)


def body(features, value_weight, output_weight, hit_list, sample_index, attention, validity):
    values = jnp.dot(features, value_weight, preferred_element_type=jnp.float32).astype(
        jnp.bfloat16
    )
    tiles = lax.axis_size("tile")
    cams = lax.axis_size("cam")
    place = lax.axis_index("cam")
    queries = sample_index.shape[0]
    width = values.shape[1]
    if cams == 2 and tiles % 4 == 0 and width == 2 * LANES and features.shape[0] % 16 == 0:
        heads = H // 2
        halves = jnp.stack([values[:, :LANES], values[:, LANES:]])
        vals = gather_values(halves, tiles)
        index = lax.dynamic_slice_in_dim(sample_index, place * heads * K, heads * K, 2)
        weights = lax.dynamic_slice_in_dim(attention, place * heads * K, heads * K, 1)
        attended = sample(hit_list, vals, index, weights, validity, heads)
        return project(attended, output_weight)
    else:
        share = queries // cams
        everything = lax.all_gather(values, ("tile", "cam"), axis=0, tiled=True)
        index, weights, valid = (
            lax.dynamic_slice_in_dim(a, place * share, share, 0)
            for a in (sample_index, attention, validity)
        )
        attended = sample(hit_list, everything, index, weights, valid, H)
    return jnp.dot(attended, output_weight, preferred_element_type=jnp.float32).astype(jnp.bfloat16)


def solution(mesh):
    in_specs = (
        P(("tile", "cam"), None),
        P(),
        P(),
        P("tile", None),
        P("tile", None, None),
        P("tile", None),
        P("tile", None),
    )
    out_specs = P(("tile", "cam"), None)
    return jax.shard_map(body, mesh=mesh, in_specs=in_specs, out_specs=out_specs, check_vma=False)
```

time: 232 us -> 52.4 us (0.23)
  the two profiles are of different devices: /device:TPU:13 before, /device:TPU:0 now
where the time goes in v1:
time: 52.4 us; the launch traced here: 52 us
  Pallas kernels  44.6 us (85%)
  other arithmetic  4.06 us (8%)
  local copies, waits for them, and re-layouts  2.25 us (4%)
  matrix products  1.12 us (2%)
    pallas_call x1, Pallas kernels, gather_values(): pl.pallas_call(functools.partial(gather_kernel, depth), out_shape=jax.Sha...  24.6 us
    pallas_call x1, Pallas kernels, sample(): pl.pallas_call(functools.partial(sample_kernel, heads), out_shape=jax.Sha...  13.8 us
    pallas_call x1, Pallas kernels, project(): pl.pallas_call(project_kernel, out_shape=jax.ShapeDtypeStruct((rows, outp...  6.22 us
    unnamed x3, local copies, waits for them, and re-layouts  1.57 us
    transpose x1, other arithmetic, sample(): attention = attention.astype(jnp.float32).T  1.38 us
    transpose x1, other arithmetic, sample(): factor = (validity.astype(jnp.float32) / count.astype(jnp.float32)).T  1.29 us
    dot_general x1, matrix products, body(): jnp.dot(features, value_weight, preferred_element_type=jnp.float32)  1.12 us

profile of v1, /device:TPU:0, one launch (start us, length us, event | category | flops | bytes accessed | tf_op | source)
XLA Modules:
  0.0 52.0 jit_solution(13682042777741754449)
XLA Ops:
  0.0 0.0 copy-start
  0.0 0.7 %reduce_sum.9 = s32[512]{0:T(512)S(1)} reduce(s32[512,2]{0,1:T(2,128)} %param.13, s32[]{:T(128)} %constant.5.clone.1), dimensions={1}, to_apply=%region_0.0 | reduce | flops 512 | bytes 6148 | tf_op jit(solution)/shard_map/reduce_sum | solution.py:225
  0.8 1.3 %divide_bitcast_fusion.factor_ref = f32[2,512]{1,0:T(2,128)} fusion(s32[512,2]{0,1:T(2,128)} %param.13, f32[512]{0:T(512)S(1)} %maximum_convert_fusion), kind=kLoop, calls=%fused_computation.5 | loop fusion | flops 2048 | bytes 10240 | tf_op jit(solution)/shard_map/transpose | solution.py:226
  2.0 1.4 %convert_bitcast_fusion.attn_ref = f32[32,512]{1,0:T(8,128)} fusion(bf16[512,64]{0,1:T(8,128)(2,1)} %param.12, s32[]{:T(128)S(6)} %select_n.4), kind=kLoop, calls=%fused_computation.2 | loop fusion | flops 16384 | bytes 98308 | tf_op jit(solution)/shard_map/transpose | solution.py:224
  3.4 1.1 %convolution_convert_fusion = bf16[192,256]{1,0:T(8,128)(2,1)S(1)} fusion(bf16[192,256]{1,0:T(8,128)(2,1)} %param.7, bf16[256,256]{1,0:T(8,128)(2,1)} %param.8), kind=kOutput, calls=%fused_computation | convolution fusion | flops 25214976 | bytes 327680 | tf_op jit(solution)/shard_map/dot_general | solution.py:287
  4.6 0.6 %pad_maximum_fusion.v_ref = bf16[2,192,128]{2,1,0:T(8,128)(2,1)} fusion(bf16[1,192,128]{2,1,0:T(8,128)(2,1)S(1)} %get-tuple-element.6, bf16[1,192,128]{2,1,0:T(8,128)(2,1)S(1)} %get-tuple-element.5), kind=kLoop, calls=%fused_computation.1 | loop fusion | flops 49152 | bytes 196608 | tf_op jit(solution)/shard_map/stack | solution.py:297
  5.2 0.0 copy-done
  5.2 0.7 %constant_dynamic-slice_fusion = s32[512,2,32]{0,2,1:T(8,128)} fusion(s32[512,2,64]{0,2,1:T(8,128)S(1)} %copy-done, s32[]{:T(128)S(6)} %select_n.4), kind=kLoop, calls=%fused_computation.7 | loop fusion | bytes 262148 | tf_op jit(solution)/shard_map/dynamic_slice | solution.py:299
  5.9 24.6 %shard_map.73.vals_ref = bf16[6144,128]{1,0:T(8,128)(2,1)} custom-call(bf16[2,192,128]{2,1,0:T(8,128)(2,1)} %pad_maximum_fusion.v_ref), custom_call_target="tpu_custom_call" | custom-call | tf_op jit(solution)/shard_map/pallas_call | solution.py:154
  30.4 13.8 %shard_map.74.a_ref = bf16[512,128]{1,0:T(8,128)(2,1)} custom-call(s32[1,2]{1,0:T(1,128)} %hit_ref.1, bf16[6144,128]{1,0:T(8,128)(2,1)} %shard_map.73.vals_ref, s32[64,512]{1,0:T(8,128)} %bitcast.13, f32[32,512]{1,0:T(8,128)} %convert_bitcast_fusion.attn_ref, f32[2,512]{1,0:T(2,128)} %divide_bitcast_fusion.factor_ref), custom_call_target="tpu_custom_call" | custom-call | tf_op jit(solution)/shard_map/pallas_call | solution.py:229
  44.2 6.2 %shard_map.75 = bf16[256,256]{1,0:T(8,128)(2,1)} custom-call(bf16[512,128]{1,0:T(8,128)(2,1)} %shard_map.74.a_ref, bf16[256,256]{1,0:T(8,128)(2,1)} %w_ref.1), custom_call_target="tpu_custom_call" | custom-call | tf_op jit(solution)/shard_map/pallas_call | solution.py:272
  50.4 1.6 %copy.9 = bf16[256,256]{1,0:T(8,128)(2,1)} copy(bf16[256,256]{1,0:T(8,128)(2,1)} %shard_map.75) | data formatting | bytes 262144
  (2 shorter events, 0.0 us)
Async XLA Ops:
  0.0 5.2 %copy-start = (s32[512,2,64]{0,2,1:T(8,128)S(1)}, s32[512,2,64]{0,2,1:T(8,128)}, u32[]{:S(2)}) copy-start(s32[512,2,64]{0,2,1:T(8,128)} %param.11) | copy-start | bytes 786436

commit v2 on v1

v2 whole, which is shorter than its diff:
```python
import functools

import jax
import jax.numpy as jnp
from jax import lax
from jax.experimental import pallas as pl
from jax.experimental.pallas import tpu as pltpu
from jax.sharding import PartitionSpec as P

H = 8
K = 8
HITS = 2
CAM_ROWS = 1024
LANES = 128
MESH = pl.DeviceIdType.MESH


def gather_kernel(depth, v_ref, G, recv, sx, sz, sy, sc):
    me = lax.axis_index("tile")
    x = lax.axis_index("cam")
    core = lax.rem(me, 2)
    y = lax.rem(me // 2, 2)
    z = me // 4
    rows, width = G.shape[0] // (depth * 8), G.shape[1]

    def half_of(index):
        return v_ref.at[:, pl.ds(pl.multiple_of(index * width, width), width)]

    def place(zz, yy, cc):
        return (zz * 2 + yy) * 2 + cc

    def block_of(zz, yy, cc, b):
        return place(zz, yy, cc) * 2 + b

    def span(blk):
        return pl.ds(pl.multiple_of(blk * rows, 16), rows)

    has_up = z < depth - 1
    has_down = z > 0
    x_peer = (me, 1 - x)
    y_peer = (place(z, 1 - y, core), x)
    c_peer = (place(z, y, 1 - core), x)
    has_up2 = z < depth - 2
    has_down2 = z > 1
    up_peer = (place(jnp.minimum(z + 1, depth - 1), y, core), x)
    down_peer = (place(jnp.maximum(z - 1, 0), y, core), x)
    up2_peer = (place(jnp.minimum(z + 2, depth - 1), y, core), x)
    down2_peer = (place(jnp.maximum(z - 2, 0), y, core), x)
    line = (
        (has_up2, up2_peer),
        (has_down2, down2_peer),
        (has_up, up_peer),
        (has_down, down_peer),
    )

    barrier = pltpu.get_barrier_semaphore()
    for peer in (x_peer, y_peer, c_peer):
        pl.semaphore_signal(barrier, inc=1, device_id=peer, device_id_type=MESH)

    peers = 3
    for exists, peer in line:
        peers = peers + exists.astype(jnp.int32)

        @pl.when(exists)
        def _(peer=peer):
            pl.semaphore_signal(barrier, inc=1, device_id=peer, device_id_type=MESH)

    pl.semaphore_wait(barrier, peers)

    def copy(src, blk, send, peer):
        return pltpu.make_async_remote_copy(
            src_ref=src,
            dst_ref=G.at[span(blk)],
            send_sem=send,
            recv_sem=recv.at[blk],
            device_id=peer,
            device_id_type=MESH,
        )

    def arrived(blk):
        copy(G.at[span(blk)], blk, sx.at[0], x_peer).wait_recv()

    own = block_of(z, y, core, x)
    copy(half_of(1 - x), own, sx.at[0], x_peer).start()

    def send_line(which, src, blk, slot):
        exists, peer = line[which]

        @pl.when(exists)
        def _():
            copy(src, blk, sz.at[slot], peer).start()

    def line_step(distance):
        for sign in (1, -1) if distance else (0,):
            zz = z - sign * distance
            live = (zz >= 0) & (zz < depth)
            for b in (0, 1):
                half = x if b == 0 else 1 - x

                def go(zz=zz, half=half, b=b, sign=sign):
                    blk = block_of(zz, y, core, half)
                    if distance == 0 and b == 0:
                        src = half_of(x)
                    else:
                        arrived(blk)
                        src = G.at[span(blk)]
                    slot = zz * 2 + half
                    if distance == 0:
                        for which in range(4):
                            send_line(which, src, blk, which * 2 + b)
                    elif distance == 2:
                        which = 2 if sign > 0 else 3
                        send_line(which, src, blk, 4 + which * 2 + b)
                    copy(src, blk, sy.at[slot], y_peer).start()
                    copy(src, blk, sc.at[slot], c_peer).start()

                if distance:
                    pl.when(live)(go)
                else:
                    go()

    def across_step(distance):
        for sign in (1, -1) if distance else (0,):
            zz = z - sign * distance
            live = (zz >= 0) & (zz < depth)
            for b in (0, 1):
                half = x if b == 0 else 1 - x

                def go(zz=zz, half=half):
                    blk = block_of(zz, 1 - y, core, half)
                    arrived(blk)
                    slot = depth * 2 + zz * 2 + half
                    copy(G.at[span(blk)], blk, sc.at[slot], c_peer).start()

                if distance:
                    pl.when(live)(go)
                else:
                    go()

    for distance in range(depth):
        line_step(distance)
        if distance:
            across_step(distance - 1)
    G[span(own), :] = v_ref[:, pl.ds(pl.multiple_of(x * width, width), width)]
    across_step(depth - 1)

    for zz in range(depth):
        for yy in (0, 1):
            for b in (0, 1):
                arrived(block_of(zz, yy, 1 - core, b))

    def sent(sem):
        copy(half_of(0), own, sem, x_peer).wait_send()

    sent(sx.at[0])
    for slot in range(depth * 2):
        sent(sy.at[slot])
    for b in (0, 1):
        for which in range(4):
            pl.when(line[which][0])(lambda i=which * 2 + b: sent(sz.at[i]))
        pl.when(has_up & has_down2)(lambda b=b: sent(sz.at[8 + b]))
        pl.when(has_down & has_up2)(lambda b=b: sent(sz.at[10 + b]))
    for slot in range(depth * 4):
        sent(sc.at[slot])


def gather_values(values, tiles):
    depth = tiles // 4
    rows, width = values.shape[0], values.shape[1] // 2
    blocks = tiles * 2
    dma = pltpu.SemaphoreType.DMA
    return pl.pallas_call(
        functools.partial(gather_kernel, depth),
        out_shape=jax.ShapeDtypeStruct((blocks * rows, width), jnp.bfloat16),
        in_specs=[pl.BlockSpec(memory_space=pltpu.VMEM)],
        out_specs=pl.BlockSpec(memory_space=pltpu.VMEM),
        scratch_shapes=[
            dma((blocks,)),
            dma((1,)),
            dma((12,)),
            dma((depth * 2,)),
            dma((depth * 4,)),
        ],
        compiler_params=pltpu.CompilerParams(collective_id=0, has_side_effects=True),
    )(values)


def lane_pick(source, index):
    return jnp.take_along_axis(source, index, axis=1, mode="promise_in_bounds")


def sample_kernel(
    heads, pair, hit_ref, head_ref, vals_ref, idx_ref, attn_ref, valid_ref, out_ref, table, attns, summed
):
    width = vals_ref.shape[1]
    head_width = width // heads
    queries = idx_ref.shape[1]
    groups = queries // LANES
    parts = CAM_ROWS // LANES
    for s in range(HITS):
        for j in range(parts):
            first = pl.multiple_of(hit_ref[0, s] * CAM_ROWS + j * LANES, LANES)
            block = vals_ref[pl.ds(first, LANES), :].astype(jnp.float32)
            table[s * parts + j] = block.T
    attns[...] = attn_ref[...].astype(jnp.float32)

    def one(step, _):
        g = step * pair // heads
        lanes = pl.ds(pl.multiple_of(g * LANES, LANES), LANES)
        valid = valid_ref[:, lanes]
        count = jnp.maximum(jnp.sum(valid, axis=0, keepdims=True), 1)
        factor = valid.astype(jnp.float32) * (1.0 / count.astype(jnp.float32))
        for e in range(pair):
            h = lax.rem(step * pair, heads) + e
            attn = attns[pl.ds(pl.multiple_of((head_ref[0] + h) * K, K), K), lanes]
            acc = [jnp.zeros((8, LANES), jnp.float32)] * (head_width // 8)
            for s in range(HITS):
                index = idx_ref[pl.ds(pl.multiple_of(s * heads * K + h * K, K), K), lanes]
                low = index & (LANES - 1)
                high = index // LANES
                weight = attn * factor[s : s + 1]
                for k in range(K):
                    lo = jnp.broadcast_to(low[k : k + 1], (8, LANES))
                    hi = jnp.broadcast_to(high[k : k + 1], (8, LANES))
                    wt = jnp.broadcast_to(weight[k : k + 1], (8, LANES))
                    masks = [hi == j for j in range(parts)]
                    for d in range(head_width // 8):
                        cols = pl.ds(pl.multiple_of(h * head_width + d * 8, 8), 8)
                        picked = lane_pick(table[s * parts, cols, :], lo)
                        for j in range(1, parts):
                            got = lane_pick(table[s * parts + j, cols, :], lo)
                            picked = jnp.where(masks[j], got, picked)
                        acc[d] = acc[d] + wt * picked
            for d in range(head_width // 8):
                summed[pl.ds(pl.multiple_of(h * head_width + d * 8, 8), 8), :] = acc[d]

        @pl.when(lax.rem(step * pair, heads) == heads - pair)
        def _():
            rows = pl.ds(pl.multiple_of(g * LANES, LANES), LANES)
            out_ref[rows, :] = summed[...].T.astype(out_ref.dtype)

        return 0

    lax.fori_loop(0, groups * heads // pair, one, 0)


def sample(hit_list, vals, index, attention, validity, heads, first_head):
    queries = index.shape[0]
    width = vals.shape[1]
    padded = -(-queries // LANES) * LANES
    index = index.reshape(queries, HITS * heads * K).T
    extra = padded - queries
    index = jnp.pad(index, ((0, 0), (0, extra)))
    validity = jnp.pad(validity.T, ((0, 0), (0, extra)))
    attention = jnp.pad(attention.T, ((0, 0), (0, extra)))
    pair = 2 if heads % 2 == 0 else 1
    first_head = jnp.reshape(first_head, (1,)).astype(jnp.int32)
    out = pl.pallas_call(
        functools.partial(sample_kernel, heads, pair),
        out_shape=jax.ShapeDtypeStruct((padded, width), jnp.bfloat16),
        in_specs=[pl.BlockSpec(memory_space=pltpu.SMEM)] * 2
        + [pl.BlockSpec(memory_space=pltpu.VMEM)] * 4,
        out_specs=pl.BlockSpec(memory_space=pltpu.VMEM),
        scratch_shapes=[
            pltpu.VMEM((HITS * CAM_ROWS // LANES, width, LANES), jnp.float32),
            pltpu.VMEM(attention.shape, jnp.float32),
            pltpu.VMEM((width, LANES), jnp.float32),
        ],
    )(hit_list, first_head, vals, index, attention, validity)
    return out[:queries]


def exchange_kernel(a_ref, out_ref, local, send, recv):
    me = lax.axis_index("tile")
    x = lax.axis_index("cam")
    rows = out_ref.shape[0]
    width = a_ref.shape[1]
    peer = (me, 1 - x)
    barrier = pltpu.get_barrier_semaphore()
    pl.semaphore_signal(barrier, inc=1, device_id=peer, device_id_type=MESH)
    pl.semaphore_wait(barrier, 1)

    def share(index):
        return a_ref.at[pl.ds(pl.multiple_of(index * rows, rows), rows)]

    mine = out_ref.at[:, pl.ds(pl.multiple_of(x * width, width), width)]
    copy = pltpu.make_async_remote_copy(
        src_ref=share(1 - x),
        dst_ref=mine,
        send_sem=send,
        recv_sem=recv,
        device_id=peer,
        device_id_type=MESH,
    )
    copy.start()
    keep = pltpu.make_async_copy(share(x), mine, local)
    keep.start()
    keep.wait()
    copy.wait()


def exchange(attended):
    queries, width = attended.shape
    dma = pltpu.SemaphoreType.DMA
    return pl.pallas_call(
        exchange_kernel,
        out_shape=jax.ShapeDtypeStruct((queries // 2, width * 2), jnp.bfloat16),
        in_specs=[pl.BlockSpec(memory_space=pltpu.VMEM)],
        out_specs=pl.BlockSpec(memory_space=pltpu.VMEM),
        scratch_shapes=[dma, dma, dma],
        compiler_params=pltpu.CompilerParams(collective_id=1, has_side_effects=True),
    )(attended)


def body(features, value_weight, output_weight, hit_list, sample_index, attention, validity):
    values = jnp.dot(features, value_weight, preferred_element_type=jnp.float32).astype(
        jnp.bfloat16
    )
    tiles = lax.axis_size("tile")
    cams = lax.axis_size("cam")
    place = lax.axis_index("cam")
    queries = sample_index.shape[0]
    width = values.shape[1]
    if cams == 2 and tiles in (4, 8, 12, 16) and width == 2 * LANES and features.shape[0] % 16 == 0:
        heads = H // 2
        vals = gather_values(values, tiles)
        index = lax.dynamic_slice_in_dim(sample_index, place * heads * K, heads * K, 2)
        attended = sample(
            hit_list, vals, index, attention, validity, heads, place * heads
        )
        attended = exchange(attended)
    else:
        share = queries // cams
        everything = lax.all_gather(values, ("tile", "cam"), axis=0, tiled=True)
        index, weights, valid = (
            lax.dynamic_slice_in_dim(a, place * share, share, 0)
            for a in (sample_index, attention, validity)
        )
        attended = sample(hit_list, everything, index, weights, valid, H, jnp.int32(0))
    return jnp.dot(attended, output_weight, preferred_element_type=jnp.float32).astype(jnp.bfloat16)


def solution(mesh):
    in_specs = (
        P(("tile", "cam"), None),
        P(),
        P(),
        P("tile", None),
        P("tile", None, None),
        P("tile", None),
        P("tile", None),
    )
    out_specs = P(("tile", "cam"), None)
    return jax.shard_map(body, mesh=mesh, in_specs=in_specs, out_specs=out_specs, check_vma=False)
```

time: 52.4 us -> 46.2 us (0.88)
  other arithmetic: 4.06 us -> 0 us
  Pallas kernels: 44.6 us -> 41.7 us
  matrix products: 1.12 us -> 3.55 us
  local copies, waits for them, and re-layouts: 2.25 us -> 0.67 us
    transpose x2 -> x0, other arithmetic: 2.66 us -> none  [the longest x1 1.38 us: sample(): attention = attention.astype(jnp.float32).T]
    pallas_call x1, Pallas kernels: 24.6 us -> 22.7 us  [gather_values(): pl.pallas_call(functools.partial(gather_kernel, depth), out_shape=jax.Sha...]
    dot_general x0 -> x1, matrix products: none -> 1.75 us  [body(): jnp.dot(attended, output_weight, preferred_element_type=jnp.float32)]
    unnamed x3 -> x4, local copies, waits for them, and re-layouts: 1.57 us -> 0.01 us
    pallas_call x2, Pallas kernels: 20 us -> 19 us  [the longest x1 13.1 us: sample(): pl.pallas_call(functools.partial(sample_kernel, heads, pair), out_shape=j...]
    reduce_sum x1 -> x0, other arithmetic: 0.75 us -> none  [sample(): count = jnp.maximum(jnp.sum(validity, axis=1, keepdims=True), 1)]
    dot_general x1, matrix products: 1.12 us -> 1.81 us  [body(): jnp.dot(features, value_weight, preferred_element_type=jnp.float32)]
    another operation x1 -> x0, other arithmetic: 0.64 us -> none  [body(): halves = jnp.stack([values[:, :LANES], values[:, LANES:]])]
where the time goes in v2:
time: 46.2 us; the launch traced here: 46 us
  Pallas kernels  41.7 us (90%)
  matrix products  3.55 us (8%)
  local copies, waits for them, and re-layouts  0.67 us (1%)
    pallas_call x1, Pallas kernels, gather_values(): pl.pallas_call(functools.partial(gather_kernel, depth), out_shape=jax.Sha...  22.7 us
    pallas_call x1, Pallas kernels, sample(): pl.pallas_call(functools.partial(sample_kernel, heads, pair), out_shape=j...  13.1 us
    pallas_call x1, Pallas kernels, exchange(): pl.pallas_call(exchange_kernel, out_shape=jax.ShapeDtypeStruct((queries /...  5.95 us
    dot_general x1, matrix products, body(): jnp.dot(features, value_weight, preferred_element_type=jnp.float32)  1.81 us
    dot_general x1, matrix products, body(): jnp.dot(attended, output_weight, preferred_element_type=jnp.float32)  1.75 us

profile of v2, /device:TPU:0, one launch (start us, length us, event | category | flops | bytes accessed | tf_op | source)
XLA Modules:
  0.0 46.0 jit_solution(9703763309143777202)
XLA Ops:
  0.0 0.0 copy-start
  0.0 1.8 %convolution_convert_fusion.1.v_ref = bf16[192,256]{1,0:T(8,128)(2,1)} fusion(bf16[192,256]{1,0:T(8,128)(2,1)} %param.7, bf16[256,256]{1,0:T(8,128)(2,1)} %param.8), kind=kOutput, calls=%fused_computation.1 | convolution fusion | flops 25214976 | bytes 327680 | tf_op jit(solution)/shard_map/dot_general | solution.py:316
  1.8 0.0 copy-done
  1.8 0.7 %constant_dynamic-slice_fusion = s32[512,2,32]{0,2,1:T(8,128)} fusion(s32[512,2,64]{0,2,1:T(8,128)S(1)} %copy-done, s32[]{:T(128)S(6)} %select_n.3), kind=kLoop, calls=%fused_computation.2 | loop fusion | bytes 262148 | tf_op jit(solution)/shard_map/dynamic_slice | solution.py:327
  2.5 0.0 copy-start.1
  2.5 22.7 %shard_map.73.vals_ref = bf16[6144,128]{1,0:T(8,128)(2,1)} custom-call(bf16[192,256]{1,0:T(8,128)(2,1)} %convolution_convert_fusion.1.v_ref), custom_call_target="tpu_custom_call" | custom-call | tf_op jit(solution)/shard_map/pallas_call | solution.py:172
  25.2 13.1 %shard_map.74.a_ref = bf16[512,128]{1,0:T(8,128)(2,1)} custom-call(s32[1,2]{1,0:T(1,128)} %hit_ref.1, s32[1]{0:T(128)} %bitcast.head_ref, bf16[6144,128]{1,0:T(8,128)(2,1)} %shard_map.73.vals_ref, s32[64,512]{1,0:T(8,128)} %bitcast.10, bf16[64,512]{1,0:T(8,128)(2,1)} %bitcast.11, s32[2,512]{1,0:T(2,128)} %bitcast.12), custom_call_target="tpu_custom_call" | custom-call | tf_op jit(solution)/shard_map/pallas_call | solution.py:258
  38.2 6.0 %shard_map.75 = bf16[256,256]{1,0:T(8,128)(2,1)} custom-call(bf16[512,128]{1,0:T(8,128)(2,1)} %shard_map.74.a_ref), custom_call_target="tpu_custom_call" | custom-call | tf_op jit(solution)/shard_map/pallas_call | solution.py:305
  44.2 0.0 copy-done.1
  44.2 1.7 %convolution_convert_fusion = bf16[256,256]{1,0:T(8,128)(2,1)} fusion(bf16[256,256]{1,0:T(8,128)(2,1)} %shard_map.75, bf16[256,256]{1,0:T(8,128)(2,1)S(1)} %copy-done.1), kind=kOutput, calls=%fused_computation | convolution fusion | flops 33619968 | bytes 393216 | tf_op jit(solution)/shard_map/dot_general | solution.py:340
Async XLA Ops:
  0.0 1.8 %copy-start = (s32[512,2,64]{0,2,1:T(8,128)S(1)}, s32[512,2,64]{0,2,1:T(8,128)}, u32[]{:S(2)}) copy-start(s32[512,2,64]{0,2,1:T(8,128)} %param.11) | copy-start | bytes 786436
  2.5 41.7 %copy-start.1 = (bf16[256,256]{1,0:T(8,128)(2,1)S(1)}, bf16[256,256]{1,0:T(8,128)(2,1)}, u32[]{:S(2)}) copy-start(bf16[256,256]{1,0:T(8,128)(2,1)} %param.9) | copy-start | bytes 393220

commit v3 on v2

--- a/solution.py
+++ b/solution.py
@@ -253,7 +253,7 @@
     index = jnp.pad(index, ((0, 0), (0, extra)))
     validity = jnp.pad(validity.T, ((0, 0), (0, extra)))
     attention = jnp.pad(attention.T, ((0, 0), (0, extra)))
-    pair = 2 if heads % 2 == 0 else 1
+    pair = 4 if heads % 4 == 0 else 1
     first_head = jnp.reshape(first_head, (1,)).astype(jnp.int32)
     out = pl.pallas_call(
         functools.partial(sample_kernel, heads, pair),

time: 46.2 us -> 45.9 us (level)
  no operation moved by 1% of the time
where the time goes in v3:
time: 45.9 us; the launch traced here: 45.7 us
  Pallas kernels  41.4 us (90%)
  matrix products  3.55 us (8%)
  local copies, waits for them, and re-layouts  0.67 us (1%)
    pallas_call x1, Pallas kernels, gather_values(): pl.pallas_call(functools.partial(gather_kernel, depth), out_shape=jax.Sha...  22.7 us
    pallas_call x1, Pallas kernels, sample(): pl.pallas_call(functools.partial(sample_kernel, heads, pair), out_shape=j...  12.8 us
    pallas_call x1, Pallas kernels, exchange(): pl.pallas_call(exchange_kernel, out_shape=jax.ShapeDtypeStruct((queries /...  5.95 us
    dot_general x1, matrix products, body(): jnp.dot(features, value_weight, preferred_element_type=jnp.float32)  1.81 us
    dot_general x1, matrix products, body(): jnp.dot(attended, output_weight, preferred_element_type=jnp.float32)  1.75 us

profile of v3, /device:TPU:0, one launch (start us, length us, event | category | flops | bytes accessed | tf_op | source)
XLA Modules:
  0.0 45.7 jit_solution(6853161792910880231)
XLA Ops:
  0.0 0.0 copy-start
  0.0 1.8 %convolution_convert_fusion.1.v_ref = bf16[192,256]{1,0:T(8,128)(2,1)} fusion(bf16[192,256]{1,0:T(8,128)(2,1)} %param.7, bf16[256,256]{1,0:T(8,128)(2,1)} %param.8), kind=kOutput, calls=%fused_computation.1 | convolution fusion | flops 25214976 | bytes 327680 | tf_op jit(solution)/shard_map/dot_general | solution.py:316
  1.8 0.0 copy-done
  1.8 0.7 %constant_dynamic-slice_fusion = s32[512,2,32]{0,2,1:T(8,128)} fusion(s32[512,2,64]{0,2,1:T(8,128)S(1)} %copy-done, s32[]{:T(128)S(6)} %select_n.3), kind=kLoop, calls=%fused_computation.2 | loop fusion | bytes 262148 | tf_op jit(solution)/shard_map/dynamic_slice | solution.py:327
  2.5 0.0 copy-start.1
  2.5 22.7 %shard_map.73.vals_ref = bf16[6144,128]{1,0:T(8,128)(2,1)} custom-call(bf16[192,256]{1,0:T(8,128)(2,1)} %convolution_convert_fusion.1.v_ref), custom_call_target="tpu_custom_call" | custom-call | tf_op jit(solution)/shard_map/pallas_call | solution.py:172
  25.2 12.8 %shard_map.74.a_ref = bf16[512,128]{1,0:T(8,128)(2,1)} custom-call(s32[1,2]{1,0:T(1,128)} %hit_ref.1, s32[1]{0:T(128)} %bitcast.head_ref, bf16[6144,128]{1,0:T(8,128)(2,1)} %shard_map.73.vals_ref, s32[64,512]{1,0:T(8,128)} %bitcast.10, bf16[64,512]{1,0:T(8,128)(2,1)} %bitcast.11, s32[2,512]{1,0:T(2,128)} %bitcast.12), custom_call_target="tpu_custom_call" | custom-call | tf_op jit(solution)/shard_map/pallas_call | solution.py:258
  38.0 6.0 %shard_map.75 = bf16[256,256]{1,0:T(8,128)(2,1)} custom-call(bf16[512,128]{1,0:T(8,128)(2,1)} %shard_map.74.a_ref), custom_call_target="tpu_custom_call" | custom-call | tf_op jit(solution)/shard_map/pallas_call | solution.py:305
  43.9 0.0 copy-done.1
  43.9 1.7 %convolution_convert_fusion = bf16[256,256]{1,0:T(8,128)(2,1)} fusion(bf16[256,256]{1,0:T(8,128)(2,1)} %shard_map.75, bf16[256,256]{1,0:T(8,128)(2,1)S(1)} %copy-done.1), kind=kOutput, calls=%fused_computation | convolution fusion | flops 33619968 | bytes 393216 | tf_op jit(solution)/shard_map/dot_general | solution.py:340
Async XLA Ops:
  0.0 1.8 %copy-start = (s32[512,2,64]{0,2,1:T(8,128)S(1)}, s32[512,2,64]{0,2,1:T(8,128)}, u32[]{:S(2)}) copy-start(s32[512,2,64]{0,2,1:T(8,128)} %param.11) | copy-start | bytes 786436
  2.5 41.5 %copy-start.1 = (bf16[256,256]{1,0:T(8,128)(2,1)S(1)}, bf16[256,256]{1,0:T(8,128)(2,1)}, u32[]{:S(2)}) copy-start(bf16[256,256]{1,0:T(8,128)(2,1)} %param.9) | copy-start | bytes 393220
